TPU v7x, 32 devices: a whole 2x2x4 slice. The times are simulated.
32 devices in a mesh: groups: 1, blk: 16 (over z, y, x), head: 2 (over core).
Axes of the slice: x: 2, y: 2, z: 4, core: 2. Of those that a mesh axis runs over, the one named last changes fastest.
Arguments:
- queries: bfloat16 [128, 8192], P(('groups', 'blk'), 'head'), may hold values from -6 to 6
- key_cache: bfloat16 [2, 32768, 8, 128], P('groups', 'blk', 'head'), may hold values from -18 to 18
- value_cache: bfloat16 [2, 32768, 8, 128], P('groups', 'blk', 'head'), may hold values from -6 to 6
- lengths: int32 [2], P('groups'), may hold values from 0 to 32704
- residual: bfloat16 [128, 8192], P('groups', 'blk'), may hold values from -6 to 6
- out_weight: bfloat16 [8192, 8192], P('head', 'blk'), may hold values from -0.0625 to 0.0625
- norm_gain: bfloat16 [8192], P('blk'), may hold values from 0.099609375 to 1.8984375
- gate_weight: bfloat16 [8192, 16384], P(None, ('head', 'blk')), may hold values from -0.0625 to 0.0625
- up_weight: bfloat16 [8192, 16384], P(None, ('head', 'blk')), may hold values from -0.0625 to 0.0625
- down_weight: bfloat16 [16384, 8192], P('head', 'blk'), may hold values from -0.046875 to 0.046875
Outputs:
- layer_out: bfloat16 [128, 8192], P('groups', 'blk')
Inputs may be any that keep to these rules, and one draw needn't show every extreme that they name: lengths[b] + 64 <= 32768; the cache holds sequence b's new keys and values at positions lengths[b] to lengths[b] + 63.
All inputs are finite; a program needn't handle non-finite values.
Results may differ from a plain program's by a relative error of at most 0.01.
Values may be sent and summed in bfloat16 or wider, within the bound.
A program may use at most 128 MiB of HBM per device.

v0:
```python
import jax
import jax.numpy as jnp
from jax import lax
from jax.sharding import PartitionSpec as P

D = 8192


neg_big = -1e30
epsilon = 1e-06


def body(
    queries,
    key_cache,
    value_cache,
    lengths,
    residual,
    out_weight,
    norm_gain,
    gate_weight,
    up_weight,
    down_weight,
):
    blocks = lax.axis_size("blk")
    my_block = lax.axis_index("blk")
    batch, ctx_dev, kv_local, head_dim = key_cache.shape
    rows_dev = queries.shape[0]
    rows_all = rows_dev * blocks
    new_tokens = rows_all // batch
    heads_local = queries.shape[1] // head_dim
    group_size = heads_local // kv_local
    all_queries = lax.all_gather(queries, "blk", axis=0, tiled=True)
    shaped = all_queries.reshape(batch, new_tokens, kv_local, group_size, head_dim)
    scores = jnp.einsum(
        "bqkgd,bckd->bqkgc", shaped, key_cache, preferred_element_type=jnp.float32
    ) * head_dim ** (-0.5)
    query_pos = lengths[:, None] + jnp.arange(new_tokens, dtype=jnp.int32)[None, :]
    key_pos = my_block * ctx_dev + jnp.arange(ctx_dev, dtype=jnp.int32)
    visible = key_pos[None, None, None, None, :] <= query_pos[:, :, None, None, None]
    block_max = jnp.max(jnp.where(visible, scores, neg_big), axis=-1)
    weights = jnp.where(visible, jnp.exp(scores - block_max[..., None]), 0.0)
    block_sum = jnp.sum(weights, axis=-1)
    block_out = jnp.einsum(
        "bqkgc,bckd->bqkgd",
        weights.astype(jnp.bfloat16),
        value_cache,
        preferred_element_type=jnp.float32,
    )
    block_mean = (block_out / jnp.maximum(block_sum, 1.0)[..., None]).astype(jnp.bfloat16)
    row_max = block_max.reshape(rows_all, heads_local)
    row_sum = block_sum.reshape(rows_all, heads_local)
    row_mean = block_mean.reshape(rows_all, heads_local, head_dim)
    got_max, got_sum = (
        lax.all_to_all(row_max[None], "blk", split_axis=1, concat_axis=0, tiled=True),
        lax.all_to_all(row_sum[None], "blk", split_axis=1, concat_axis=0, tiled=True),
    )
    got_mean = lax.all_to_all(row_mean[None], "blk", split_axis=1, concat_axis=0, tiled=True)
    top = jnp.max(got_max, axis=0)
    factor = got_sum * jnp.exp(got_max - top[None])
    total_sum = jnp.sum(factor, axis=0)
    total_out = jnp.sum(got_mean.astype(jnp.float32) * factor[..., None], axis=0)
    attn = (
        (total_out / total_sum[..., None])
        .astype(jnp.bfloat16)
        .reshape(rows_dev, heads_local * head_dim)
    )
    proj_part = jnp.dot(
        lax.all_gather(attn, "blk", axis=0, tiled=True),
        out_weight,
        preferred_element_type=jnp.float32,
    )
    projected = lax.psum(proj_part.astype(jnp.bfloat16), "head").astype(jnp.float32)
    stream = residual.astype(jnp.float32) + projected
    squares = lax.psum(jnp.sum(stream * stream, axis=1), "blk")
    normed = (
        stream * lax.rsqrt(squares / D + epsilon)[:, None] * norm_gain.astype(jnp.float32)[None, :]
    ).astype(jnp.bfloat16)
    piece = lax.all_gather(normed, "blk", axis=1, tiled=True)
    gate = jnp.dot(piece, gate_weight, preferred_element_type=jnp.float32)
    up = jnp.dot(piece, up_weight, preferred_element_type=jnp.float32)
    hidden = (jax.nn.silu(gate) * up).astype(jnp.bfloat16)
    down_part = jnp.dot(
        lax.all_gather(hidden, "blk", axis=1, tiled=True),
        down_weight,
        preferred_element_type=jnp.float32,
    )
    down_total = lax.psum(down_part.astype(jnp.bfloat16), "head").astype(jnp.float32)
    return (stream + down_total).astype(jnp.bfloat16)


def solution(mesh):
    in_specs = (
        P(("groups", "blk"), "head"),
        P("groups", "blk", "head", None),
        P("groups", "blk", "head", None),
        P("groups"),
        P("groups", "blk"),
        P("head", "blk"),
        P("blk"),
        P(None, ("head", "blk")),
        P(None, ("head", "blk")),
        P("head", "blk"),
    )
    out_specs = P("groups", "blk")
    return jax.shard_map(body, mesh=mesh, in_specs=in_specs, out_specs=out_specs, check_vma=False)
```

profile of v0, /device:TPU:0, one launch (start us, length us, event | category | flops | bytes accessed | tf_op | source)
XLA Modules:
  0.0 444.1 jit_solution(5362369163561286765)
XLA Ops:
  8.2 59.7 %all-gather.5.cloned.1.call-done = bf16[128,4096]{1,0:T(8,128)(2,1)} async-done(((bf16[8,4096]{1,0:T(8,128)(2,1)}), bf16[128,4096]{1,0:T(8,128)(2,1)}) %all-gather.5.cloned.1.call-update) | async-done | bytes 1048592 | tf_op jit(solution)/shard_map/all_gather | solution.py:33
  67.9 1.5 copy.45
  69.4 17.1 %fusion = (f32[2,64,4,8]{1,3,2,0:T(8,128)S(1)}, f32[2,4,2048,64,8]{2,3,4,1,0:T(8,128)}) fusion(pred[2,64,2048]{2,1,0:T(8,128)(4,1)S(1)} %broadcast_compare_fusion, bf16[2,64,4,8,128]{4,3,2,1,0:T(8,128)(2,1)S(1)} %bitcast.53, bf16[2,2048,4,128,1]{3,2,1,0,4:T(4,128)(2,1)} %bitcast.55), kind=kOutput, calls=%fused_computation.2 | convolution fusion | flops 2172645376 | bytes 39075840 | tf_op jit(solution)/shard_map/bqkgd,bckd->bqkgc/dot_general | solution.py:35
  86.5 15.1 %fusion.3 = f32[2,64,4,8]{1,3,2,0:T(8,128)S(1)} fusion(f32[2,4,2048,64,8]{2,3,4,1,0:T(8,128)} %get-tuple-element.8, f32[2,64,4,8]{1,3,2,0:T(8,128)S(1)} %get-tuple-element.7, pred[2,64,2048]{2,1,0:T(8,128)(4,1)S(1)} %broadcast_compare_fusion), kind=kLoop, calls=%fused_computation.5 | loop fusion | flops 33550336 | bytes 33849344 | tf_op jit(solution)/shard_map/reduce_sum | solution.py:43
  103.8 4.4 %all-to-all-start.2 = ((f32[16,1,256]{2,1,0:T(1,128)}), f32[16,1,256]{2,1,0:T(1,128)S(1)}, u32[]{:S(2)}, u32[]{:S(2)}) async-start(f32[16,1,256]{2,1,0:T(1,128)} %reshape.82), calls=%async_computation.2 | async-start | bytes 32768 | tf_op jit(solution)/shard_map/all_to_all | solution.py:55
  110.0 5.6 %all-to-all-done.2 = f32[16,1,256]{2,1,0:T(1,128)S(1)} async-done(((f32[16,1,256]{2,1,0:T(1,128)}), f32[16,1,256]{2,1,0:T(1,128)S(1)}, u32[]{:S(2)}, u32[]{:S(2)}) %all-to-all-start.2) | async-done | bytes 16416 | tf_op jit(solution)/shard_map/all_to_all | solution.py:55
  115.6 3.5 all-to-all-start.1
  119.1 15.6 %fusion.12 = bf16[2,64,4,8,128]{4,1,3,2,0:T(8,128)(2,1)S(1)} fusion(bf16[2,2048,4,128,1]{3,2,1,0,4:T(4,128)(2,1)} %bitcast.63, f32[2,4,2048,64,8]{2,3,4,1,0:T(8,128)} %get-tuple-element.8, f32[2,64,4,8]{1,3,2,0:T(8,128)S(1)} %get-tuple-element.7, pred[2,64,2048]{2,1,0:T(8,128)(4,1)S(1)} %broadcast_compare_fusion, f32[2,64,4,8]{1,3,2,0:T(8,128)S(1)} %broadcast_maximum_fusion), kind=kOutput, calls=%fused_computation.15 | convolution fusion | flops 2182086656 | bytes 39092224 | tf_op jit(solution)/shard_map/bqkgc,bckd->bqkgd/dot_general | solution.py:44
  134.8 1.7 copy.33
  136.4 6.9 %all-to-all-start = ((bf16[1,128,32,128]{3,2,0,1:T(8,128)(2,1)}), bf16[1,128,32,128]{3,2,0,1:T(8,128)(2,1)S(1)}, u32[]{:S(2)}, u32[]{:S(2)}) async-start(bf16[1,128,32,128]{3,2,0,1:T(8,128)(2,1)} %bitcast.5), calls=%async_computation | async-start | bytes 2097152 | tf_op jit(solution)/shard_map/all_to_all | solution.py:58
  145.2 19.7 %all-to-all-done = bf16[1,128,32,128]{3,2,0,1:T(8,128)(2,1)S(1)} async-done(((bf16[1,128,32,128]{3,2,0,1:T(8,128)(2,1)}), bf16[1,128,32,128]{3,2,0,1:T(8,128)(2,1)S(1)}, u32[]{:S(2)}, u32[]{:S(2)}) %all-to-all-start) | async-done | bytes 1048608 | tf_op jit(solution)/shard_map/all_to_all | solution.py:58
  166.5 54.4 %all-gather.7.cloned.1.call-done = bf16[128,4096]{1,0:T(8,128)(2,1)} async-done(((bf16[8,4096]{1,0:T(8,128)(2,1)}), bf16[128,4096]{1,0:T(8,128)(2,1)}) %all-gather.7.cloned.1.call-update) | async-done | bytes 1048592 | tf_op jit(solution)/shard_map/all_gather | solution.py:69
  220.9 3.9 convolution_convert_fusion
  224.9 16.8 %all-reduce.3.cloned.1.call-done = bf16[128,512]{1,0:T(8,128)(2,1)} async-done(((bf16[128,512]{1,0:T(8,128)(2,1)}), bf16[128,512]{1,0:T(8,128)(2,1)}) %all-reduce.3.cloned.1.call-update) | async-done | bytes 131088 | tf_op jit(solution)/shard_map/psum | solution.py:73
  241.7 1.0 multiply_reduce_fusion
  242.7 42.0 %psum.22 = f32[128]{0:T(128)S(1)} all-reduce(f32[128]{0:T(128)S(1)} %multiply_reduce_fusion), channel_id=1, replica_groups=mesh['groups'=1,'blk'=16,'head'=2] {'blk'}, use_global_device_ids=true, to_apply=%region_7.8 | all-reduce | flops 128 | bytes 1024 | tf_op jit(solution)/shard_map/psum | solution.py:75
  284.7 1.7 multiply_convert_fusion
  286.5 56.9 %all-gather.9.cloned.1.call-done = bf16[128,8192]{1,0:T(8,128)(2,1)} async-done(((bf16[128,512]{1,0:T(8,128)(2,1)}), bf16[128,8192]{1,0:T(8,128)(2,1)}) %all-gather.9.cloned.1.call-update) | async-done | bytes 2097168 | tf_op jit(solution)/shard_map/all_gather | solution.py:79
  343.3 5.4 %fusion.23 = f32[128,512]{1,0:T(8,128)S(1)} fusion(bf16[128,8192]{1,0:T(8,128)(2,1)} %all-gather.9.cloned.1.call-done, bf16[8192,512]{1,0:T(8,128)(2,1)} %param.17), kind=kOutput, calls=%fused_computation.37 | convolution fusion | flops 1073741824 | bytes 10747904 | tf_op jit(solution)/shard_map/dot_general | solution.py:80
  348.7 5.4 %fusion.17 = bf16[128,512]{1,0:T(8,128)(2,1)} fusion(bf16[128,8192]{1,0:T(8,128)(2,1)S(1)} %copy-done, bf16[8192,512]{1,0:T(8,128)(2,1)} %param.18, f32[128,512]{1,0:T(8,128)S(1)} %fusion.23), kind=kOutput, calls=%fused_computation.17 | convolution fusion | flops 1074135040 | bytes 10878976 | tf_op jit(solution)/shard_map/dot_general | solution.py:81
  354.3 59.2 %all-gather.11.cloned.1.call-done = bf16[128,8192]{1,0:T(8,128)(2,1)} async-done(((bf16[128,512]{1,0:T(8,128)(2,1)}), bf16[128,8192]{1,0:T(8,128)(2,1)}) %all-gather.11.cloned.1.call-update) | async-done | bytes 2097168 | tf_op jit(solution)/shard_map/all_gather | solution.py:84
  413.4 5.9 %convolution_convert_fusion.1 = bf16[128,512]{1,0:T(8,128)(2,1)} fusion(bf16[128,8192]{1,0:T(8,128)(2,1)} %all-gather.11.cloned.1.call-done, bf16[8192,512]{1,0:T(8,128)(2,1)} %param.19), kind=kOutput, calls=%fused_computation.19 | convolution fusion | flops 1073807360 | bytes 10616832 | tf_op jit(solution)/shard_map/dot_general | solution.py:83
  419.4 16.2 %all-reduce.5.cloned.1.call-done = bf16[128,512]{1,0:T(8,128)(2,1)} async-done(((bf16[128,512]{1,0:T(8,128)(2,1)}), bf16[128,512]{1,0:T(8,128)(2,1)}) %all-reduce.5.cloned.1.call-update) | async-done | bytes 131088 | tf_op jit(solution)/shard_map/psum | solution.py:88
  435.6 1.6 add_convert_fusion
  (47 shorter events, 9.2 us)
Async XLA Ops:
  6.5 61.4 %all-gather.5.cloned.1.call-start = ((), (), s32[]{:S(2)}) async-start(), calls=%async_computation.3 | async-start | bytes 1114112 | tf_op jit(solution)/shard_map/all_gather | solution.py:33
  103.8 11.8 %all-to-all-start.2 = ((f32[16,1,256]{2,1,0:T(1,128)}), f32[16,1,256]{2,1,0:T(1,128)S(1)}, u32[]{:S(2)}, u32[]{:S(2)}) async-start(f32[16,1,256]{2,1,0:T(1,128)} %reshape.82), calls=%async_computation.2 | async-start | bytes 32768 | tf_op jit(solution)/shard_map/all_to_all | solution.py:55
  115.6 20.8 %all-to-all-start.1 = ((f32[16,1,256]{2,1,0:T(1,128)}), f32[16,1,256]{2,1,0:T(1,128)S(1)}, u32[]{:S(2)}, u32[]{:S(2)}) async-start(f32[16,1,256]{2,1,0:T(1,128)} %reshape.80), calls=%async_computation.1 | async-start | bytes 32768 | tf_op jit(solution)/shard_map/all_to_all | solution.py:56
  134.7 90.1 %copy-start.3 = (bf16[512]{0:T(512)(128)(2,1)S(1)}, bf16[512]{0:T(512)(128)(2,1)}, u32[]{:S(2)}) copy-start(bf16[512]{0:T(512)(128)(2,1)} %param.16) | copy-start | bytes 3076
  134.7 106.9 %copy-start.1 = (bf16[128,512]{1,0:T(8,128)(2,1)S(1)}, bf16[128,512]{1,0:T(8,128)(2,1)}, u32[]{:S(2)}) copy-start(bf16[128,512]{1,0:T(8,128)(2,1)} %param.14) | copy-start | bytes 393220
  136.4 28.5 %all-to-all-start = ((bf16[1,128,32,128]{3,2,0,1:T(8,128)(2,1)}), bf16[1,128,32,128]{3,2,0,1:T(8,128)(2,1)S(1)}, u32[]{:S(2)}, u32[]{:S(2)}) async-start(bf16[1,128,32,128]{3,2,0,1:T(8,128)(2,1)} %bitcast.5), calls=%async_computation | async-start | bytes 2097152 | tf_op jit(solution)/shard_map/all_to_all | solution.py:58
  143.3 77.6 %all-gather.7.cloned.1.call-start = ((), (), s32[]{:S(2)}) async-start(), calls=%async_computation.4 | async-start | bytes 1114112 | tf_op jit(solution)/shard_map/all_gather | solution.py:69
  166.4 75.2 %all-reduce.3.cloned.1.call-start = ((), (), s32[]{:S(2)}) async-start(), calls=%async_computation.5 | async-start | bytes 262144 | tf_op jit(solution)/shard_map/psum | solution.py:73
  224.8 118.5 %all-gather.9.cloned.1.call-start = ((), (), s32[]{:S(2)}) async-start(), calls=%async_computation.6 | async-start | bytes 2228224 | tf_op jit(solution)/shard_map/all_gather | solution.py:79
  286.4 127.0 %all-gather.11.cloned.1.call-start = ((), (), s32[]{:S(2)}) async-start(), calls=%async_computation.7 | async-start | bytes 2228224 | tf_op jit(solution)/shard_map/all_gather | solution.py:84
  343.3 5.4 %copy-start = (bf16[128,8192]{1,0:T(8,128)(2,1)S(1)}, bf16[128,8192]{1,0:T(8,128)(2,1)}, u32[]{:S(2)}) copy-start(bf16[128,8192]{1,0:T(8,128)(2,1)} %all-gather.9.cloned.1.call-done) | copy-start | bytes 6291460
  354.2 81.4 %copy-start.2 = (bf16[128,512]{1,0:T(8,128)(2,1)S(1)}, bf16[128,512]{1,0:T(8,128)(2,1)}, u32[]{:S(2)}) copy-start(bf16[128,512]{1,0:T(8,128)(2,1)} %all-reduce.3.cloned.1.call-done) | copy-start | bytes 393220
  354.2 81.4 %all-reduce.5.cloned.1.call-start = ((), (), s32[]{:S(2)}) async-start(), calls=%async_computation.8 | async-start | bytes 262144 | tf_op jit(solution)/shard_map/psum | solution.py:88
Sparse Core Ops, SparseCore 0:
  10.1 57.7 all-gather.4
  166.6 54.2 all-gather.6
  224.9 16.7 all-reduce.2
  286.5 56.7 all-gather.8
  354.3 59.0 all-gather.10
  419.5 16.0 all-reduce.4
where the time goes:
time: 445 us; the launch traced here: 444 us
  waiting for transfers between devices  289 us (65%)
  matrix products  53.4 us (12%)
  blocking collectives  42 us (9%)
  other arithmetic  24 us (5%)
  starting transfers between devices  15.2 us (3%)
  between operations  13.7 us (3%)
  local copies, waits for them, and re-layouts  6.46 us (1%)
    all_gather x1, waiting for transfers between devices, body(): all_queries = lax.all_gather(queries, 'blk', axis=0, tiled=True)  59.7 us
    all_gather x1, waiting for transfers between devices, body(): lax.all_gather(hidden, 'blk', axis=1, tiled=True)  59.2 us
    all_gather x1, waiting for transfers between devices, body(): piece = lax.all_gather(normed, 'blk', axis=1, tiled=True)  56.9 us
    all_gather x1, waiting for transfers between devices, body(): lax.all_gather(attn, 'blk', axis=0, tiled=True)  54.4 us
    psum x1, blocking collectives, body(): squares = lax.psum(jnp.sum(stream * stream, axis=1), 'blk')  42 us
    all_to_all x1, waiting for transfers between devices, body(): lax.all_to_all(row_mean[None], 'blk', split_axis=1, concat_axis=0, tiled=...  19.7 us
    dot_general x1, matrix products, body(): jnp.einsum('bqkgd,bckd->bqkgc', shaped, key_cache, preferred_element_type...  17.1 us
    psum x1, waiting for transfers between devices, body(): lax.psum(proj_part.astype(jnp.bfloat16), 'head').astype(jnp.float32)  16.8 us
  transfers between devices with their start and end apart: 9, of which 8 were waited for; matrix products, arithmetic and copies ran while one was open for 5% of the time, Pallas kernels for 0%

commit v1 on v0

--- a/solution.py
+++ b/solution.py
@@ -1,6 +1,11 @@
+import functools
+import math
+
 import jax
 import jax.numpy as jnp
 from jax import lax
+from jax.experimental import pallas as pl
+from jax.experimental.pallas import tpu as pltpu
 from jax.sharding import PartitionSpec as P
 
 D = 8192
@@ -89,6 +94,428 @@
     return (stream + down_total).astype(jnp.bfloat16)
 
 
+MESH = pl.DeviceIdType.MESH
+BF = jnp.bfloat16
+F32 = jnp.float32
+
+
+def remote(src, dst, ssem, rsem, **where):
+    return pltpu.make_async_remote_copy(
+        src_ref=src, dst_ref=dst, send_sem=ssem, recv_sem=rsem, device_id=where, device_id_type=MESH
+    )
+
+
+def enter(n, me, head):
+    barrier = pltpu.get_barrier_semaphore()
+    for k in range(1, n):
+        pl.semaphore_signal(
+            barrier, inc=1, device_id={"blk": lax.rem(me + k, n)}, device_id_type=MESH
+        )
+    pl.semaphore_signal(barrier, inc=1, device_id={"head": 1 - head}, device_id_type=MESH)
+    pl.semaphore_wait(barrier, n)
+
+
+def start_if(cond, copy):
+    if cond is None:
+        copy.start()
+    else:
+        pl.when(cond)(copy.start)
+
+
+def gather(buf, parts, ssem, rsem, n, me, forward=None):
+    depth = n // 4
+    z = me // 4
+    x_peer = me + 1 - 2 * (me % 2)
+    y_peer = me + 2 - 4 * ((me // 2) % 2)
+    sends = []
+
+    def send(part, slot, block, target, cond=None):
+        copy = remote(
+            buf.at[part, block], buf.at[part, block], ssem.at[part, slot], rsem.at[part, block], blk=target
+        )
+        start_if(cond, copy)
+        sends.append((cond, copy))
+
+    def pass_on(part, block, cond=None):
+        if forward is not None:
+            head, fsem = forward
+            copy = remote(
+                buf.at[part, block], buf.at[part, block], fsem.at[block], rsem.at[part, block], head=1 - head
+            )
+            start_if(cond, copy)
+            sends.append((cond, copy))
+
+    def arrived(part, block, cond=None):
+        copy = remote(
+            buf.at[part, block], buf.at[part, block], ssem.at[part, 0], rsem.at[part, block], blk=x_peer
+        )
+        if cond is None:
+            copy.wait_recv()
+        else:
+            pl.when(cond)(copy.wait_recv)
+
+    def peers(first):
+        return x_peer * (1 - first) + y_peer * first, y_peer * (1 - first) + x_peer * first
+
+    for part, first in parts:
+        near, far = peers(first)
+        send(part, 0, me, me + 4, z < depth - 1)
+        send(part, 1, me, me - 4, z > 0)
+        send(part, 2, me, near)
+        send(part, 3, me, far)
+        pass_on(part, me)
+    slot = 4
+    for d in range(1, depth):
+        for step in (4, -4):
+            for part, first in parts:
+                near, far = peers(first)
+                block = me - step * d
+                if step > 0:
+                    here = z >= d
+                    more = jnp.logical_and(z >= d, z < depth - 1)
+                else:
+                    here = z < depth - d
+                    more = jnp.logical_and(z < depth - d, z > 0)
+                arrived(part, block, here)
+                send(part, slot, block, me + step, more)
+                send(part, slot + 1, block, near, here)
+                send(part, slot + 2, block, far, here)
+                pass_on(part, block, here)
+            slot += 3
+    for k in range(depth):
+        zz = lax.rem(z + k, depth)
+        for part, first in parts:
+            near, far = peers(first)
+            block = near + 4 * (zz - z)
+            arrived(part, block)
+            send(part, slot, block, far)
+            pass_on(part, block)
+        slot += 1
+    for k in range(depth):
+        zz = lax.rem(z + k, depth)
+        for part, first in parts:
+            near, far = peers(first)
+            for block in (far + 4 * (zz - z), near + far - me + 4 * (zz - z)):
+                arrived(part, block)
+                pass_on(part, block)
+    if forward is not None:
+        head = forward[0]
+        for i in range(n):
+            arrived(1 - head, i)
+
+    def finish():
+        for cond, copy in sends:
+            if cond is None:
+                copy.wait_send()
+            else:
+                pl.when(cond)(copy.wait_send)
+
+    return finish
+
+
+def slots(n):
+    depth = n // 4
+    return 4 + 6 * (depth - 1) + depth
+
+
+def swap(part, mine, theirs, ssem, rsem, head):
+    mine[...] = part.astype(BF)
+    copy = remote(mine, theirs, ssem, rsem, head=1 - head)
+    copy.start()
+    copy.wait()
+    return mine[...].astype(F32) + theirs[...].astype(F32)
+
+
+def attend(
+    n, lengths, q, keys, values, residual, gain, ow,
+    stream_out, scaled_out, squares_out,
+    qbuf, kraw, vraw, wide, kd, vd, qs, osend, orecv, stat, statr, abuf, ow_v, acc, mine, theirs,
+    qss, qrs, oss, ors, tss, trs, ass, ars, loc, xss, xrs,
+):
+    me = lax.axis_index("blk")
+    head = lax.axis_index("head")
+    batch, flat, hd = kraw.shape
+    kv = kd.shape[0] // batch
+    ctx = flat // kv
+    rows_dev, width = q.shape
+    half = width // 2
+    per = half // hd
+    group = width // hd // kv
+    owners = n // batch
+    tokens = owners * rows_dev
+    kcopy = pltpu.make_async_copy(keys, kraw, loc.at[0])
+    vcopy = pltpu.make_async_copy(values, vraw, loc.at[1])
+    wcopy = pltpu.make_async_copy(ow, ow_v, loc.at[2])
+    qcopies = [
+        pltpu.make_async_copy(q.at[:, pl.ds(p * half, half)], qbuf.at[p, me], loc.at[3 + p])
+        for p in range(2)
+    ]
+    for c in qcopies:
+        c.start()
+    kcopy.start()
+    vcopy.start()
+    wcopy.start()
+    enter(n, me, head)
+    for c in qcopies:
+        c.wait()
+    finish_q = gather(qbuf, [(0, 0), (1, 1)], qss, qrs, n, me)
+    kcopy.wait()
+    vcopy.wait()
+    for raw, out in ((kraw, kd), (vraw, vd)):
+        for b in range(batch):
+            wide[...] = raw[b].astype(F32)
+            for h in range(kv):
+                out[b * kv + h] = wide[pl.ds(h, ctx, stride=kv), :].astype(BF)
+    for b in range(batch):
+        for j in range(kv * group):
+            val = qbuf[j // per, b * owners : (b + 1) * owners, :, (j % per) * hd : (j % per + 1) * hd]
+            val = val.astype(F32).reshape(tokens, hd).astype(BF)
+            h, g = j // group, j % group
+            qs[b * kv + h, g * tokens : (g + 1) * tokens] = val
+    scale = hd ** (-0.5) * math.log2(math.e)
+    gt = 4
+    tile = gt * tokens
+    lane = lax.broadcasted_iota(jnp.int32, (owners, rows_dev, 128), 2)
+
+    def one(bh, carry):
+        b, h = bh // kv, bh % kv
+        limit = lengths[b] - me * ctx
+        for rt in range(group // gt):
+            s = lax.dot_general(
+                qs[bh, rt * tile : (rt + 1) * tile], kd[bh], (((1,), (1,)), ((), ())), preferred_element_type=F32
+            ) * scale
+            row = lax.broadcasted_iota(jnp.int32, (tile, 1), 0) % tokens
+            col = lax.broadcasted_iota(jnp.int32, (tile, ctx), 1)
+            s = jnp.where(col <= row + limit, s, neg_big)
+            m = jnp.max(s, axis=1, keepdims=True)
+            p = jnp.exp2(s - jnp.maximum(m, -1e29))
+            l = jnp.sum(p, axis=1, keepdims=True)
+            o = jnp.dot(p.astype(BF), vd[bh], preferred_element_type=F32)
+            o = o / jnp.maximum(l, 1.0)
+            for g in range(gt):
+                gg = rt * gt + g
+                cut = slice(g * tokens, (g + 1) * tokens)
+                piece = o[cut].reshape(owners, rows_dev, hd).astype(BF)
+                osend[h, pl.ds(b * owners, owners), :, gg * hd : (gg + 1) * hd] = piece
+                at = h * group + gg
+                for which, col_value in ((0, m), (1, l)):
+                    old = stat[pl.ds(b * owners, owners), which]
+                    new = jnp.broadcast_to(col_value[cut], (tokens, 128)).reshape(owners, rows_dev, 128)
+                    stat[pl.ds(b * owners, owners), which] = jnp.where(lane == at, new, old)
+        for j in range(owners):
+            to = b * owners + j
+            copy = remote(osend.at[h, to], orecv.at[h, me], oss.at[h, to], ors.at[h, me], blk=to)
+            start_if(to != me, copy)
+        return carry
+
+    stat[...] = jnp.zeros_like(stat)
+    lax.fori_loop(0, batch * kv, one, 0)
+    for to in range(n):
+        start_if(to != me, remote(stat.at[to], statr.at[me], tss.at[to], trs.at[me], blk=to))
+    own = [pltpu.make_async_copy(stat.at[me], statr.at[me], loc.at[3])]
+    own += [pltpu.make_async_copy(osend.at[h, me], orecv.at[h, me], loc.at[5 + h]) for h in range(kv)]
+    for c in own:
+        c.start()
+    finish_q()
+    for c in own:
+        c.wait()
+    for i in range(n):
+        for h in range(kv):
+            copy = remote(osend.at[h, i], orecv.at[h, i], oss.at[h, i], ors.at[h, i], blk=i)
+            pl.when(i != me)(copy.wait)
+        pl.when(i != me)(remote(stat.at[i], statr.at[i], tss.at[i], trs.at[i], blk=i).wait)
+    maxima = statr[:, 0]
+    top = jnp.max(maxima, axis=0)
+    factor = statr[:, 1] * jnp.exp2(maxima - top[None])
+    total = jnp.sum(factor, axis=0)
+    for j in range(kv * group):
+        h, g = j // group, j % group
+        out = jnp.sum(
+            orecv[h, :, :, g * hd : (g + 1) * hd].astype(F32) * factor[:, :, j : j + 1], axis=0
+        ) / total[:, j : j + 1]
+        abuf[j // per, me, :, (j % per) * hd : (j % per + 1) * hd] = out.astype(BF)
+    finish_a = gather(abuf, [(0, 0), (1, 1)], ass, ars, n, me)
+    wcopy.wait()
+    acc[...] = jnp.zeros_like(acc)
+    chunk = 512
+    for p in range(2):
+        def proj(c, carry, p=p):
+            at = pl.multiple_of(c * chunk, chunk)
+            lhs = abuf[p, :, :, pl.ds(at, chunk)].astype(F32).reshape(n * rows_dev, chunk).astype(BF)
+            acc[...] += jnp.dot(lhs, ow_v[pl.ds(p * half + at, chunk), :], preferred_element_type=F32)
+            return carry
+        lax.fori_loop(0, half // chunk, proj, 0)
+    finish_a()
+    stream = residual[...].astype(F32) + swap(acc[...], mine, theirs, xss, xrs, head)
+    stream_out[...] = stream
+    scaled = (stream * gain[...].astype(F32)).astype(BF)
+    cut = scaled.shape[1] // 2
+    scaled_out[0] = scaled[:, :cut]
+    scaled_out[1] = scaled[:, cut:]
+    squares_out[...] = lax.dot_general(
+        jnp.ones((8, stream.shape[1]), F32), stream * stream, (((1,), (1,)), ((), ())),
+        precision=lax.Precision.HIGHEST, preferred_element_type=F32,
+    )
+
+
+def feed(
+    n, stream, scaled, squares, gw, uw, dw, out,
+    sbuf, sqbuf, hbuf, gv, uv, dv, gacc, uacc, mine, theirs,
+    sss, srs, sfs, qss, qrs, hss, hrs, loc, xss, xrs,
+):
+    me = lax.axis_index("blk")
+    head = lax.axis_index("head")
+    weights = [pltpu.make_async_copy(a, b, loc.at[i]) for i, (a, b) in enumerate(((gw, gv), (uw, uv), (dw, dv)))]
+    own = pltpu.make_async_copy(scaled.at[head], sbuf.at[head, me], loc.at[3])
+    own_sq = pltpu.make_async_copy(squares, sqbuf.at[me], loc.at[4])
+    own.start()
+    own_sq.start()
+    for c in weights:
+        c.start()
+    enter(n, me, head)
+    own.wait()
+    own_sq.wait()
+    for i in range(n):
+        start_if(i != me, remote(sqbuf.at[me], sqbuf.at[me], qss.at[i], qrs.at[me], blk=i))
+    finish_s = gather(sbuf, [(head, head)], sss, srs, n, me, forward=(head, sfs))
+    for i in range(n):
+        pl.when(i != me)(remote(sqbuf.at[i], sqbuf.at[i], qss.at[i], qrs.at[i], blk=i).wait)
+    cut = sbuf.shape[3]
+    unroll = 4
+
+    def product(buf, pairs):
+        for acc, _ in pairs:
+            acc[...] = jnp.zeros_like(acc)
+
+        def step(c, carry):
+            for acc, w in pairs:
+                total = None
+                for k in range(unroll):
+                    for p in range(2):
+                        i = c * unroll + k
+                        at = pl.multiple_of(i * 2 * cut + p * cut, cut)
+                        term = jnp.dot(buf[p, i], w[pl.ds(at, cut), :], preferred_element_type=F32)
+                        total = term if total is None else total + term
+                acc[...] += total
+            return carry
+
+        lax.fori_loop(0, n // unroll, step, 0)
+
+    weights[0].wait()
+    weights[1].wait()
+    product(sbuf, ((gacc, gv), (uacc, uv)))
+    total = jnp.sum(sqbuf[...], axis=0)
+    width = gacc.shape[1]
+    spread = lax.dot_general(
+        total, jnp.full((8, width), 0.125, F32), (((0,), (0,)), ((), ())),
+        precision=lax.Precision.HIGHEST, preferred_element_type=F32,
+    )
+    scale = lax.rsqrt(spread / (n * stream.shape[1]) + epsilon)
+    gate = gacc[...] * scale
+    hidden = ((gate / (1.0 + jnp.exp(-gate))) * (uacc[...] * scale)).astype(BF)
+    hbuf[0, me] = hidden[:, :cut]
+    hbuf[1, me] = hidden[:, cut:]
+    finish_h = gather(hbuf, [(0, 0), (1, 1)], hss, hrs, n, me)
+    weights[2].wait()
+    product(hbuf, ((gacc, dv),))
+    out[...] = (stream[...] + swap(gacc[...], mine, theirs, xss, xrs, head)).astype(BF)
+    finish_s()
+    finish_h()
+
+
+VM = pl.BlockSpec(memory_space=pltpu.VMEM)
+HBM = pl.BlockSpec(memory_space=pl.ANY)
+DMA = pltpu.SemaphoreType.DMA
+
+
+def kernel_body(
+    queries, key_cache, value_cache, lengths, residual, out_weight, norm_gain, gate_weight, up_weight, down_weight
+):
+    n = lax.axis_size("blk")
+    batch, ctx, kv, hd = key_cache.shape
+    rows_dev, width = queries.shape
+    half = width // 2
+    group = width // hd // kv
+    rows, cols = residual.shape
+    keys = key_cache.reshape(batch, ctx * kv, hd)
+    values = value_cache.reshape(batch, ctx * kv, hd)
+    block = (n, rows_dev, group * hd)
+    s = slots(n)
+    stream, scaled, squares = pl.pallas_call(
+        functools.partial(attend, n),
+        out_shape=(
+            jax.ShapeDtypeStruct((rows, cols), F32),
+            jax.ShapeDtypeStruct((2, rows, cols // 2), BF),
+            jax.ShapeDtypeStruct((8, rows), F32),
+        ),
+        in_specs=[pl.BlockSpec(memory_space=pltpu.SMEM), VM, HBM, HBM, VM, VM, HBM],
+        out_specs=(VM, VM, VM),
+        scratch_shapes=[
+            pltpu.VMEM((2, n, rows_dev, half), BF),
+            pltpu.VMEM(keys.shape, BF),
+            pltpu.VMEM(keys.shape, BF),
+            pltpu.VMEM(keys.shape[1:], F32),
+            pltpu.VMEM((batch * kv, ctx, hd), BF),
+            pltpu.VMEM((batch * kv, ctx, hd), BF),
+            pltpu.VMEM((batch * kv, group * rows // batch, hd), BF),
+            pltpu.VMEM((kv,) + block, BF),
+            pltpu.VMEM((kv,) + block, BF),
+            pltpu.VMEM((n, 2, rows_dev, 128), F32),
+            pltpu.VMEM((n, 2, rows_dev, 128), F32),
+            pltpu.VMEM((2, n, rows_dev, half), BF),
+            pltpu.VMEM(out_weight.shape, BF),
+            pltpu.VMEM((rows, cols), F32),
+            pltpu.VMEM((rows, cols), BF),
+            pltpu.VMEM((rows, cols), BF),
+            DMA((2, s)), DMA((2, n)), DMA((kv, n)), DMA((kv, n)), DMA((n,)), DMA((n,)),
+            DMA((2, s)), DMA((2, n)), DMA((5 + kv,)), DMA, DMA,
+        ],
+        compiler_params=pltpu.CompilerParams(
+            collective_id=0, has_side_effects=True, vmem_limit_bytes=60 * 1024 * 1024
+        ),
+        name="attend",
+    )(lengths, queries, keys, values, residual, norm_gain.reshape(1, -1), out_weight)
+    units = gate_weight.shape[1]
+    return pl.pallas_call(
+        functools.partial(feed, n),
+        out_shape=jax.ShapeDtypeStruct((rows, cols), BF),
+        in_specs=[VM, VM, VM, HBM, HBM, HBM],
+        out_specs=VM,
+        scratch_shapes=[
+            pltpu.VMEM((2, n, rows, cols // 2), BF),
+            pltpu.VMEM((n, 8, rows), F32),
+            pltpu.VMEM((2, n, rows, units // 2), BF),
+            pltpu.VMEM(gate_weight.shape, BF),
+            pltpu.VMEM(up_weight.shape, BF),
+            pltpu.VMEM(down_weight.shape, BF),
+            pltpu.VMEM((rows, units), F32),
+            pltpu.VMEM((rows, units), F32),
+            pltpu.VMEM((rows, cols), BF),
+            pltpu.VMEM((rows, cols), BF),
+            DMA((2, s)), DMA((2, n)), DMA((n,)), DMA((n,)), DMA((n,)),
+            DMA((2, s)), DMA((2, n)), DMA((5,)), DMA, DMA,
+        ],
+        compiler_params=pltpu.CompilerParams(
+            collective_id=1, has_side_effects=True, vmem_limit_bytes=60 * 1024 * 1024
+        ),
+        name="feed",
+    )(stream, scaled, squares, gate_weight, up_weight, down_weight)
+
+
+def pick(*args):
+    queries, key_cache, residual, gate_weight = args[0], args[1], args[4], args[7]
+    n = lax.axis_size("blk")
+    fits = (
+        n % 8 == 0
+        and queries.shape[0] == 8
+        and n % key_cache.shape[0] == 0
+        and residual.shape[1] % 256 == 0
+        and residual.shape[1] == gate_weight.shape[1]
+        and residual.shape[0] == 128
+    )
+    return kernel_body(*args) if fits else body(*args)
+
+
 def solution(mesh):
     in_specs = (
         P(("groups", "blk"), "head"),
@@ -103,4 +530,4 @@
         P("head", "blk"),
     )
     out_specs = P("groups", "blk")
-    return jax.shard_map(body, mesh=mesh, in_specs=in_specs, out_specs=out_specs, check_vma=False)
+    return jax.shard_map(pick, mesh=mesh, in_specs=in_specs, out_specs=out_specs, check_vma=False)

time: 445 us -> 140 us (0.31)
  waiting for transfers between devices: 289 us -> 0 us
  Pallas kernels: 0 us -> 137 us
  matrix products: 53.4 us -> 0 us
  blocking collectives: 42 us -> 0 us
  other arithmetic: 24 us -> 0 us
  starting transfers between devices: 15.2 us -> 0 us
  between operations: 13.7 us -> 0.02 us
    all_gather x4 -> x0, waiting for transfers between devices: 230 us -> none  [the longest x1 59.7 us: body(): all_queries = lax.all_gather(queries, 'blk', axis=0, tiled=True)]
    pallas_call x0 -> x2, Pallas kernels: none -> 137 us  [the longest x1 84.3 us: kernel_body(): pl.pallas_call(functools.partial(attend, n), out_shape=(jax.ShapeDtypeStr...]
    dot_general x6 -> x0, matrix products: 53.4 us -> none  [the longest x1 17.1 us: body(): jnp.einsum('bqkgd,bckd->bqkgc', shaped, key_cache, preferred_element_type...]
    psum x1 -> x0, blocking collectives: 42 us -> none  [body(): squares = lax.psum(jnp.sum(stream * stream, axis=1), 'blk')]
    psum x2 -> x0, waiting for transfers between devices: 33.1 us -> none  [the longest x1 16.8 us: body(): lax.psum(proj_part.astype(jnp.bfloat16), 'head').astype(jnp.float32)]
    all_to_all x3 -> x0, waiting for transfers between devices: 25.4 us -> none  [the longest x1 19.7 us: body(): lax.all_to_all(row_mean[None], 'blk', split_axis=1, concat_axis=0, tiled=...]
    reduce_sum x4 -> x0, other arithmetic: 16.9 us -> none  [the longest x1 15.1 us: body(): block_sum = jnp.sum(weights, axis=-1)]
    all_to_all x3 -> x0, starting transfers between devices: 14.8 us -> none  [the longest x1 6.87 us: body(): lax.all_to_all(row_mean[None], 'blk', split_axis=1, concat_axis=0, tiled=...]
  transfers between devices with their start and end apart: 9 -> 0, of which waited for: 8 -> 0; matrix products, arithmetic and copies ran while one was open for 5% -> 0% of each run, Pallas kernels for 0% -> 0%
where the time goes in v1:
time: 140 us
  Pallas kernels  137 us (98%)
  local copies, waits for them, and re-layouts  2.83 us (2%)
    pallas_call x1, Pallas kernels, kernel_body(): pl.pallas_call(functools.partial(attend, n), out_shape=(jax.ShapeDtypeStr...  84.3 us
    pallas_call x1, Pallas kernels, kernel_body(): pl.pallas_call(functools.partial(feed, n), out_shape=jax.ShapeDtypeStruct...  52.9 us

profile of v1, /device:TPU:0, one launch (start us, length us, event | category | flops | bytes accessed | tf_op | source)
XLA Modules:
  0.0 140.0 jit_solution(8771011811420280348)
XLA Ops:
  0.0 1.3 reshape.11.gain
  1.3 84.3 %attend.1 = (f32[128,512]{1,0:T(8,128)}, bf16[2,128,256]{2,1,0:T(8,128)(2,1)}, f32[8,128]{1,0:T(8,128)}) custom-call(s32[2]{0:T(128)} %lengths.1, bf16[8,4096]{1,0:T(8,128)(2,1)} %q.1, bf16[2,8192,128]{2,1,0:T(8,128)(2,1)} %bitcast.2, bf16[2,8192,128]{2,1,0:T(8,128)(2,1)} %bitcast.3, bf16[128,512]{1,0:T(8,128)(2,1)} %residual.1, ...), custom_call_target="tpu_custom_call" | custom-call | tf_op jit(solution)/shard_map/attend/pallas_call | solution.py:444
  85.5 52.9 %feed.1 = bf16[128,512]{1,0:T(8,128)(2,1)} custom-call(f32[128,512]{1,0:T(8,128)} %get-tuple-element.8.stream, bf16[2,128,256]{2,1,0:T(8,128)(2,1)} %get-tuple-element.9.scaled, f32[8,128]{1,0:T(8,128)} %get-tuple-element.10.squares, bf16[8192,512]{1,0:T(8,128)(2,1)} %gw.1, bf16[8192,512]{1,0:T(8,128)(2,1)} %uw.1, bf16[8192,512]{1,0:T(8,128)(2,1)} %dw.1), custom_call_target="tpu_custom_call" | custom-call | tf_op jit(solution)/shard_map/feed/pallas_call | solution.py:479
  138.4 1.6 %copy.12 = bf16[128,512]{1,0:T(8,128)(2,1)} copy(bf16[128,512]{1,0:T(8,128)(2,1)} %feed.1) | data formatting | bytes 262144

commit v2 on v1

v2 whole, which is shorter than its diff:
```python
import functools
import math

import jax
import jax.numpy as jnp
from jax import lax
from jax.experimental import pallas as pl
from jax.experimental.pallas import tpu as pltpu
from jax.sharding import PartitionSpec as P

D = 8192


neg_big = -1e30
epsilon = 1e-06


def body(
    queries,
    key_cache,
    value_cache,
    lengths,
    residual,
    out_weight,
    norm_gain,
    gate_weight,
    up_weight,
    down_weight,
):
    blocks = lax.axis_size("blk")
    my_block = lax.axis_index("blk")
    batch, ctx_dev, kv_local, head_dim = key_cache.shape
    rows_dev = queries.shape[0]
    rows_all = rows_dev * blocks
    new_tokens = rows_all // batch
    heads_local = queries.shape[1] // head_dim
    group_size = heads_local // kv_local
    all_queries = lax.all_gather(queries, "blk", axis=0, tiled=True)
    shaped = all_queries.reshape(batch, new_tokens, kv_local, group_size, head_dim)
    scores = jnp.einsum(
        "bqkgd,bckd->bqkgc", shaped, key_cache, preferred_element_type=jnp.float32
    ) * head_dim ** (-0.5)
    query_pos = lengths[:, None] + jnp.arange(new_tokens, dtype=jnp.int32)[None, :]
    key_pos = my_block * ctx_dev + jnp.arange(ctx_dev, dtype=jnp.int32)
    visible = key_pos[None, None, None, None, :] <= query_pos[:, :, None, None, None]
    block_max = jnp.max(jnp.where(visible, scores, neg_big), axis=-1)
    weights = jnp.where(visible, jnp.exp(scores - block_max[..., None]), 0.0)
    block_sum = jnp.sum(weights, axis=-1)
    block_out = jnp.einsum(
        "bqkgc,bckd->bqkgd",
        weights.astype(jnp.bfloat16),
        value_cache,
        preferred_element_type=jnp.float32,
    )
    block_mean = (block_out / jnp.maximum(block_sum, 1.0)[..., None]).astype(jnp.bfloat16)
    row_max = block_max.reshape(rows_all, heads_local)
    row_sum = block_sum.reshape(rows_all, heads_local)
    row_mean = block_mean.reshape(rows_all, heads_local, head_dim)
    got_max, got_sum = (
        lax.all_to_all(row_max[None], "blk", split_axis=1, concat_axis=0, tiled=True),
        lax.all_to_all(row_sum[None], "blk", split_axis=1, concat_axis=0, tiled=True),
    )
    got_mean = lax.all_to_all(row_mean[None], "blk", split_axis=1, concat_axis=0, tiled=True)
    top = jnp.max(got_max, axis=0)
    factor = got_sum * jnp.exp(got_max - top[None])
    total_sum = jnp.sum(factor, axis=0)
    total_out = jnp.sum(got_mean.astype(jnp.float32) * factor[..., None], axis=0)
    attn = (
        (total_out / total_sum[..., None])
        .astype(jnp.bfloat16)
        .reshape(rows_dev, heads_local * head_dim)
    )
    proj_part = jnp.dot(
        lax.all_gather(attn, "blk", axis=0, tiled=True),
        out_weight,
        preferred_element_type=jnp.float32,
    )
    projected = lax.psum(proj_part.astype(jnp.bfloat16), "head").astype(jnp.float32)
    stream = residual.astype(jnp.float32) + projected
    squares = lax.psum(jnp.sum(stream * stream, axis=1), "blk")
    normed = (
        stream * lax.rsqrt(squares / D + epsilon)[:, None] * norm_gain.astype(jnp.float32)[None, :]
    ).astype(jnp.bfloat16)
    piece = lax.all_gather(normed, "blk", axis=1, tiled=True)
    gate = jnp.dot(piece, gate_weight, preferred_element_type=jnp.float32)
    up = jnp.dot(piece, up_weight, preferred_element_type=jnp.float32)
    hidden = (jax.nn.silu(gate) * up).astype(jnp.bfloat16)
    down_part = jnp.dot(
        lax.all_gather(hidden, "blk", axis=1, tiled=True),
        down_weight,
        preferred_element_type=jnp.float32,
    )
    down_total = lax.psum(down_part.astype(jnp.bfloat16), "head").astype(jnp.float32)
    return (stream + down_total).astype(jnp.bfloat16)


MESH = pl.DeviceIdType.MESH
BF = jnp.bfloat16
F32 = jnp.float32


def remote(src, dst, ssem, rsem, **where):
    return pltpu.make_async_remote_copy(
        src_ref=src, dst_ref=dst, send_sem=ssem, recv_sem=rsem, device_id=where, device_id_type=MESH
    )


def enter(n, me, head):
    barrier = pltpu.get_barrier_semaphore()
    for k in range(1, n):
        pl.semaphore_signal(
            barrier, inc=1, device_id={"blk": lax.rem(me + k, n)}, device_id_type=MESH
        )
    pl.semaphore_signal(barrier, inc=1, device_id={"head": 1 - head}, device_id_type=MESH)
    pl.semaphore_wait(barrier, n)


def start_if(cond, copy):
    if cond is None:
        copy.start()
    else:
        pl.when(cond)(copy.start)


def gather(buf, parts, ssem, rsem, n, me, forward=None, work=(), visit=None):
    depth = n // 4
    z = me // 4
    x_peer = me + 1 - 2 * (me % 2)
    y_peer = me + 2 - 4 * ((me // 2) % 2)
    sends = []

    def send(part, slot, block, target, cond=None):
        copy = remote(
            buf.at[part, block], buf.at[part, block], ssem.at[part, slot], rsem.at[part, block], blk=target
        )
        start_if(cond, copy)
        sends.append((cond, copy))

    def pass_on(part, block, cond=None):
        if forward is not None:
            head, fsem = forward
            copy = remote(
                buf.at[part, block], buf.at[part, block], fsem.at[block], rsem.at[part, block], head=1 - head
            )
            start_if(cond, copy)
            sends.append((cond, copy))

    def arrived(part, block, cond=None):
        copy = remote(
            buf.at[part, block], buf.at[part, block], ssem.at[part, 0], rsem.at[part, block], blk=x_peer
        )
        if cond is None:
            copy.wait_recv()
        else:
            pl.when(cond)(copy.wait_recv)

    def peers(first):
        return x_peer * (1 - first) + y_peer * first, y_peer * (1 - first) + x_peer * first

    for part, first in parts:
        near, far = peers(first)
        send(part, 0, me, me + 4, z < depth - 1)
        send(part, 1, me, me - 4, z > 0)
        send(part, 2, me, near)
        send(part, 3, me, far)
        pass_on(part, me)
    work = list(work)
    if work:
        work.pop(0)()
    slot = 4
    for d in range(1, depth):
        for step in (4, -4):
            for part, first in parts:
                near, far = peers(first)
                block = me - step * d
                if step > 0:
                    here = z >= d
                    more = jnp.logical_and(z >= d, z < depth - 1)
                else:
                    here = z < depth - d
                    more = jnp.logical_and(z < depth - d, z > 0)
                arrived(part, block, here)
                send(part, slot, block, me + step, more)
                send(part, slot + 1, block, near, here)
                send(part, slot + 2, block, far, here)
                pass_on(part, block, here)
            slot += 3
        if work:
            work.pop(0)()
    for k in range(depth):
        zz = lax.rem(z + k, depth)
        for part, first in parts:
            near, far = peers(first)
            block = near + 4 * (zz - z)
            arrived(part, block)
            send(part, slot, block, far)
            pass_on(part, block)
        slot += 1
    if work:
        work.pop(0)()
    others = [] if forward is None else [(1 - p, 1 - f) for p, f in parts]
    for group in (parts, others):
        items = []
        for k in range(depth):
            shift = 4 * (lax.rem(z + k, depth) - z)
            for part, first in group:
                near, far = peers(first)
                if group is others:
                    arrived(part, me + shift)
                    arrived(part, near + shift)
                items += [(part, me + shift), (part, near + shift)]
        if visit is not None and items:
            visit(items)
    for k in range(depth):
        shift = 4 * (lax.rem(z + k, depth) - z)
        items = []
        for mine, (part, first) in [(True, p) for p in parts] + [(False, p) for p in others]:
            near, far = peers(first)
            for block in (far + shift, near + far - me + shift):
                arrived(part, block)
                if mine:
                    pass_on(part, block)
                items.append((part, block))
        if visit is not None:
            visit(items)

    def finish():
        for cond, copy in sends:
            if cond is None:
                copy.wait_send()
            else:
                pl.when(cond)(copy.wait_send)

    return finish


def slots(n):
    depth = n // 4
    return 4 + 6 * (depth - 1) + depth


def swap(part, mine, theirs, ssem, rsem, head):
    mine[...] = part.astype(BF)
    copy = remote(mine, theirs, ssem, rsem, head=1 - head)
    copy.start()
    copy.wait()
    return mine[...].astype(F32) + theirs[...].astype(F32)


def layer(
    n, lengths, q, keys, values, residual, gain, ow, gw, uw, dw, out,
    qbuf, raw, wide, kd, vd, qs, osend, orecv, stat, ssend, srecv, abuf, sbuf, sqbuf, hbuf,
    ow_v, gv, uv, dv, stream, acc, gacc, mine, theirs,
    qss, qrs, oss, ors, tss, trs, ass, ars, sss, srs, sfs, nss, nrs, hss, hrs, loc, wsem, xss, xrs,
):
    me = lax.axis_index("blk")
    head = lax.axis_index("head")
    batch, flat, hd = raw.shape
    kv = kd.shape[0] // batch
    ctx = flat // kv
    rows_dev, width = q.shape
    half = width // 2
    per = half // hd
    group = width // hd // kv
    owners = n // batch
    tokens = owners * rows_dev
    rows = batch * tokens
    wcopies = [
        pltpu.make_async_copy(a, b, wsem.at[i])
        for i, (a, b) in enumerate(((ow, ow_v), (gw, gv), (uw, uv), (dw, dv)))
    ]
    qcopies = [
        pltpu.make_async_copy(q.at[:, pl.ds(p * half, half)], qbuf.at[p, me], loc.at[p]) for p in range(2)
    ]
    for c in qcopies:
        c.start()
    kcopies = [pltpu.make_async_copy(keys.at[b], raw.at[b], loc.at[2 + b]) for b in range(batch)]
    vcopies = [pltpu.make_async_copy(values.at[b], raw.at[b], loc.at[2 + b]) for b in range(batch)]
    for c in kcopies:
        c.start()
    enter(n, me, head)
    for c in qcopies:
        c.wait()

    def spread_heads(dest, b, copies, after):
        def run():
            copies[b].wait()
            part = wide.shape[0]
            for c in range(flat // part):
                wide[...] = raw[b, c * part : (c + 1) * part].astype(F32)
                for h in range(kv):
                    dest[b * kv + h, c * part // kv : (c + 1) * part // kv] = wide[
                        pl.ds(h, part // kv, stride=kv), :
                    ].astype(BF)
            for c in after:
                c.start()
        return run

    jobs = []
    for b in range(batch):
        jobs.append(spread_heads(kd, b, kcopies, [vcopies[b]]))
    for b in range(batch):
        jobs.append(spread_heads(vd, b, vcopies, wcopies if b == batch - 1 else []))
    finish_q = gather(qbuf, [(0, 0), (1, 1)], qss, qrs, n, me, work=jobs)
    for b in range(batch):
        for j in range(kv * group):
            val = qbuf[j // per, b * owners : (b + 1) * owners, :, (j % per) * hd : (j % per + 1) * hd]
            val = val.astype(F32).reshape(tokens, hd).astype(BF)
            h, g = j // group, j % group
            qs[b * kv + h, g * tokens : (g + 1) * tokens] = val
    scale = hd ** (-0.5) * math.log2(math.e)
    gt = 4
    tile = gt * tokens
    share = n // kv
    heads_each = group // share
    lane = lax.broadcasted_iota(jnp.int32, (tokens, 128), 1)
    z = me // 4

    def one(b, h):
        bh = b * kv + h
        limit = lengths[b] - me * ctx
        first_row = pl.multiple_of(b * tokens, tokens)
        stats = jnp.zeros((tokens, 128), F32)
        for rt in range(group // gt):
            s = lax.dot_general(
                qs[bh, rt * tile : (rt + 1) * tile], kd[bh], (((1,), (1,)), ((), ())), preferred_element_type=F32
            ) * scale
            row = lax.broadcasted_iota(jnp.int32, (tile, 1), 0) % tokens
            col = lax.broadcasted_iota(jnp.int32, (tile, ctx), 1)
            s = jnp.where(col <= row + limit, s, neg_big)
            m = jnp.max(s, axis=1, keepdims=True)
            p = jnp.exp2(s - jnp.maximum(m, -1e29))
            l = jnp.sum(p, axis=1, keepdims=True)
            o = jnp.dot(p.astype(BF), vd[bh], preferred_element_type=F32)
            o = (o / jnp.maximum(l, 1.0)).astype(BF)
            for g in range(gt):
                j, e = divmod(rt * gt + g, heads_each)
                cut = slice(g * tokens, (g + 1) * tokens)
                osend[h * share + j, pl.ds(first_row, tokens), e * hd : (e + 1) * hd] = o[cut]
                stats = jnp.where(lane == j * 8 + e, m[cut], stats)
                stats = jnp.where(lane == 64 + j * 8 + e, l[cut], stats)
            for j in range(rt * gt // heads_each, (rt + 1) * gt // heads_each):
                to = h * share + j
                copy = remote(
                    osend.at[to, pl.ds(first_row, tokens)], orecv.at[me, pl.ds(first_row, tokens)],
                    oss.at[b, to], ors.at[b, me], blk=to,
                )
                start_if(to != me, copy)
        stat[pl.ds(first_row, tokens)] = stats

    def plane(k, carry):
        h = lax.rem(z + kv - 1 - k, kv)

        def each(b, c):
            one(b, h)
            return c

        lax.fori_loop(0, batch, each, 0)
        turned = stat[...].T
        for j in range(share):
            to = h * share + j
            for which in range(2):
                ssend[to, which] = turned[which * 64 + j * 8 : which * 64 + j * 8 + 8]
            start_if(to != me, remote(ssend.at[to], srecv.at[me], tss.at[to], trs.at[me], blk=to))
        return carry

    lax.fori_loop(0, kv, plane, 0)
    own = [
        pltpu.make_async_copy(ssend.at[me], srecv.at[me], loc.at[0]),
        pltpu.make_async_copy(osend.at[me], orecv.at[me], loc.at[1]),
    ]
    for c in own:
        c.start()
    finish_q()
    for c in own:
        c.wait()
    for i in range(n):
        for b in range(batch):
            cut = pl.ds(b * tokens, tokens)
            copy = remote(osend.at[i, cut], orecv.at[i, cut], oss.at[b, i], ors.at[b, i], blk=i)
            pl.when(i != me)(copy.wait)
        pl.when(i != me)(remote(ssend.at[i], srecv.at[i], tss.at[i], trs.at[i], blk=i).wait)
    maxima = srecv[:, 0]
    top = jnp.max(maxima, axis=0)
    factor = srecv[:, 1] * jnp.exp2(maxima - top[None])
    ratio = (factor / jnp.sum(factor, axis=0)[None]).reshape(n * 8, rows).T
    for e in range(heads_each):
        total = jnp.zeros((rows, hd), F32)
        for i in range(n):
            total += orecv[i, :, e * hd : (e + 1) * hd].astype(F32) * ratio[:, i * 8 + e : i * 8 + e + 1]
        abuf[e, me] = total.astype(BF)

    def products(buf, pairs):
        cut = buf.shape[3]

        def visit(items):
            for c in range(0, len(items), 4):
                for total, w in pairs:
                    term = total[...]
                    for part, block in items[c : c + 4]:
                        at = pl.multiple_of(block * (2 * cut) + part * cut, cut)
                        term += jnp.dot(buf[part, block], w[pl.ds(at, cut), :], preferred_element_type=F32)
                    total[...] = term
        return visit

    acc[...] = jnp.zeros_like(acc)
    for c in wcopies:
        c.wait()
    finish_a = gather(abuf, [(0, 0), (1, 1)], ass, ars, n, me, visit=products(abuf, ((acc, ow_v),)))
    new = residual[...].astype(F32) + swap(acc[...], mine.at[0], theirs.at[0], xss.at[0], xrs.at[0], head)
    stream[...] = new
    scaled = (new * gain[...].astype(F32)).astype(BF)
    cut = scaled.shape[1] // 2
    for p in range(2):
        @pl.when(head == p)
        def _(p=p):
            sbuf[p, me] = scaled[:, p * cut : (p + 1) * cut]
    sqbuf[me] = lax.dot_general(
        jnp.ones((8, new.shape[1]), F32), new * new, (((1,), (1,)), ((), ())),
        precision=lax.Precision.HIGHEST, preferred_element_type=F32,
    )
    acc[...] = jnp.zeros_like(acc)
    gacc[...] = jnp.zeros_like(gacc)
    for i in range(n):
        start_if(i != me, remote(sqbuf.at[me], sqbuf.at[me], nss.at[i], nrs.at[me], blk=i))
    finish_s = gather(
        sbuf, [(head, head)], sss, srs, n, me, forward=(head, sfs),
        visit=products(sbuf, ((gacc, gv), (acc, uv))),
    )
    for i in range(n):
        pl.when(i != me)(remote(sqbuf.at[i], sqbuf.at[i], nss.at[i], nrs.at[i], blk=i).wait)
    spread = lax.dot_general(
        jnp.sum(sqbuf[...], axis=0), jnp.full((8, gacc.shape[1]), 0.125, F32), (((0,), (0,)), ((), ())),
        precision=lax.Precision.HIGHEST, preferred_element_type=F32,
    )
    norm = lax.rsqrt(spread / (n * stream.shape[1]) + epsilon)
    gate = gacc[...] * norm
    hidden = ((gate / (1.0 + jnp.exp(-gate))) * (acc[...] * norm)).astype(BF)
    cut = hidden.shape[1] // 2
    hbuf[0, me] = hidden[:, :cut]
    hbuf[1, me] = hidden[:, cut:]
    acc[...] = jnp.zeros_like(acc)
    finish_h = gather(hbuf, [(0, 0), (1, 1)], hss, hrs, n, me, visit=products(hbuf, ((acc, dv),)))
    down = swap(acc[...], mine.at[1], theirs.at[1], xss.at[1], xrs.at[1], head)
    out[...] = (stream[...] + down).astype(BF)
    finish_a()
    finish_s()
    finish_h()


VM = pl.BlockSpec(memory_space=pltpu.VMEM)
HBM = pl.BlockSpec(memory_space=pl.ANY)
DMA = pltpu.SemaphoreType.DMA


def kernel_body(
    queries, key_cache, value_cache, lengths, residual, out_weight, norm_gain, gate_weight, up_weight, down_weight
):
    n = lax.axis_size("blk")
    batch, ctx, kv, hd = key_cache.shape
    rows_dev, width = queries.shape
    half = width // 2
    group = width // hd // kv
    rows, cols = residual.shape
    keys = key_cache.reshape(batch, ctx * kv, hd)
    values = value_cache.reshape(batch, ctx * kv, hd)
    s = slots(n)
    units = gate_weight.shape[1]
    return pl.pallas_call(
        functools.partial(layer, n),
        out_shape=jax.ShapeDtypeStruct((rows, cols), BF),
        in_specs=[pl.BlockSpec(memory_space=pltpu.SMEM), VM, HBM, HBM, VM, VM, HBM, HBM, HBM, HBM],
        out_specs=VM,
        scratch_shapes=[
            pltpu.VMEM((2, n, rows_dev, half), BF),
            pltpu.VMEM(keys.shape, BF),
            pltpu.VMEM((ctx * kv // 4, hd), F32),
            pltpu.VMEM((batch * kv, ctx, hd), BF),
            pltpu.VMEM((batch * kv, ctx, hd), BF),
            pltpu.VMEM((batch * kv, group * rows // batch, hd), BF),
            pltpu.VMEM((n, rows, width // n), BF),
            pltpu.VMEM((n, rows, width // n), BF),
            pltpu.VMEM((rows, 128), F32),
            pltpu.VMEM((n, 2, 8, rows), F32),
            pltpu.VMEM((n, 2, 8, rows), F32),
            pltpu.VMEM((2, n, rows, hd), BF),
            pltpu.VMEM((2, n, rows, cols // 2), BF),
            pltpu.VMEM((n, 8, rows), F32),
            pltpu.VMEM((2, n, rows, units // 2), BF),
            pltpu.VMEM(out_weight.shape, BF),
            pltpu.VMEM(gate_weight.shape, BF),
            pltpu.VMEM(up_weight.shape, BF),
            pltpu.VMEM(down_weight.shape, BF),
            pltpu.VMEM((rows, cols), F32),
            pltpu.VMEM((rows, cols), F32),
            pltpu.VMEM((rows, units), F32),
            pltpu.VMEM((2, rows, cols), BF),
            pltpu.VMEM((2, rows, cols), BF),
            DMA((2, s)), DMA((2, n)), DMA((batch, n)), DMA((batch, n)), DMA((n,)), DMA((n,)),
            DMA((2, s)), DMA((2, n)), DMA((2, s)), DMA((2, n)), DMA((n,)), DMA((n,)), DMA((n,)),
            DMA((2, s)), DMA((2, n)), DMA((2 + batch,)), DMA((4,)), DMA((2,)), DMA((2,)),
        ],
        compiler_params=pltpu.CompilerParams(
            collective_id=0, has_side_effects=True, vmem_limit_bytes=67_043_328
        ),
        name="layer",
    )(
        lengths, queries, keys, values, residual, norm_gain.reshape(1, -1),
        out_weight, gate_weight, up_weight, down_weight,
    )


def pick(*args):
    queries, key_cache, residual, gate_weight = args[0], args[1], args[4], args[7]
    n = lax.axis_size("blk")
    fits = (
        n == 4 * key_cache.shape[2]
        and queries.shape[0] == 8
        and queries.shape[1] == 256 * n
        and key_cache.shape[3] == 128
        and n % key_cache.shape[0] == 0
        and residual.shape[1] % 256 == 0
        and residual.shape[1] == gate_weight.shape[1]
        and residual.shape[0] == 128
    )
    return kernel_body(*args) if fits else body(*args)


def solution(mesh):
    in_specs = (
        P(("groups", "blk"), "head"),
        P("groups", "blk", "head", None),
        P("groups", "blk", "head", None),
        P("groups"),
        P("groups", "blk"),
        P("head", "blk"),
        P("blk"),
        P(None, ("head", "blk")),
        P(None, ("head", "blk")),
        P("head", "blk"),
    )
    out_specs = P("groups", "blk")
    return jax.shard_map(pick, mesh=mesh, in_specs=in_specs, out_specs=out_specs, check_vma=False)
```

time: 140 us -> 124 us (0.89)
  Pallas kernels: 137 us -> 121 us
    pallas_call x2 -> x1, Pallas kernels: 137 us -> 121 us  [kernel_body(): pl.pallas_call(functools.partial(layer, n), out_shape=jax.ShapeDtypeStruc...]
where the time goes in v2:
time: 124 us; the launch traced here: 123 us
  Pallas kernels  121 us (98%)
  local copies, waits for them, and re-layouts  2.83 us (2%)
    pallas_call x1, Pallas kernels, kernel_body(): pl.pallas_call(functools.partial(layer, n), out_shape=jax.ShapeDtypeStruc...  121 us

profile of v2, /device:TPU:0, one launch (start us, length us, event | category | flops | bytes accessed | tf_op | source)
XLA Modules:
  0.0 123.4 jit_solution(4611676100110123205)
XLA Ops:
  0.0 1.3 %reshape.11.gain = bf16[1,512]{1,0:T(2,128)(2,1)} reshape(bf16[512]{0:T(512)(128)(2,1)} %param.16) | data formatting | bytes 2048 | tf_op jit(solution)/shard_map/reshape | solution.py:508
  1.3 120.6 %layer.1 = bf16[128,512]{1,0:T(8,128)(2,1)} custom-call(s32[2]{0:T(128)} %lengths.1, bf16[8,4096]{1,0:T(8,128)(2,1)} %q.1, bf16[2,8192,128]{2,1,0:T(8,128)(2,1)} %bitcast.2, bf16[2,8192,128]{2,1,0:T(8,128)(2,1)} %bitcast.3, bf16[128,512]{1,0:T(8,128)(2,1)} %residual.1, bf16[1,512]{1,0:T(2,128)(2,1)} %reshape.11.gain, bf16[4096,512]{1,0:T(8,128)(2,1)} %ow.1, ...), custom_call_target="tpu_custom_call" | custom-call | tf_op jit(solution)/shard_map/layer/pallas_call | solution.py:469
  121.9 1.6 %copy.12 = bf16[128,512]{1,0:T(8,128)(2,1)} copy(bf16[128,512]{1,0:T(8,128)(2,1)} %layer.1) | data formatting | bytes 262144

commit v3 on v2

--- a/solution.py
+++ b/solution.py
@@ -251,7 +251,7 @@
     n, lengths, q, keys, values, residual, gain, ow, gw, uw, dw, out,
     qbuf, raw, wide, kd, vd, qs, osend, orecv, stat, ssend, srecv, abuf, sbuf, sqbuf, hbuf,
     ow_v, gv, uv, dv, stream, acc, gacc, mine, theirs,
-    qss, qrs, oss, ors, tss, trs, ass, ars, sss, srs, sfs, nss, nrs, hss, hrs, loc, wsem, xss, xrs,
+    gss, qrs, oss, ors, tss, trs, ars, srs, nrs, hrs, loc, wsem, xss, xrs,
 ):
     me = lax.axis_index("blk")
     head = lax.axis_index("head")
@@ -301,7 +301,7 @@
         jobs.append(spread_heads(kd, b, kcopies, [vcopies[b]]))
     for b in range(batch):
         jobs.append(spread_heads(vd, b, vcopies, wcopies if b == batch - 1 else []))
-    finish_q = gather(qbuf, [(0, 0), (1, 1)], qss, qrs, n, me, work=jobs)
+    finish_q = gather(qbuf, [(0, 0), (1, 1)], gss, qrs, n, me, work=jobs)
     for b in range(batch):
         for j in range(kv * group):
             val = qbuf[j // per, b * owners : (b + 1) * owners, :, (j % per) * hd : (j % per + 1) * hd]
@@ -406,29 +406,28 @@
     acc[...] = jnp.zeros_like(acc)
     for c in wcopies:
         c.wait()
-    finish_a = gather(abuf, [(0, 0), (1, 1)], ass, ars, n, me, visit=products(abuf, ((acc, ow_v),)))
+    finish_a = gather(abuf, [(0, 0), (1, 1)], gss, ars, n, me, visit=products(abuf, ((acc, ow_v),)))
     new = residual[...].astype(F32) + swap(acc[...], mine.at[0], theirs.at[0], xss.at[0], xrs.at[0], head)
     stream[...] = new
     scaled = (new * gain[...].astype(F32)).astype(BF)
     cut = scaled.shape[1] // 2
     for p in range(2):
-        @pl.when(head == p)
-        def _(p=p):
-            sbuf[p, me] = scaled[:, p * cut : (p + 1) * cut]
+        sbuf[p, me] = scaled[:, p * cut : (p + 1) * cut]
     sqbuf[me] = lax.dot_general(
         jnp.ones((8, new.shape[1]), F32), new * new, (((1,), (1,)), ((), ())),
         precision=lax.Precision.HIGHEST, preferred_element_type=F32,
     )
     acc[...] = jnp.zeros_like(acc)
     gacc[...] = jnp.zeros_like(gacc)
+    finish_a()
     for i in range(n):
-        start_if(i != me, remote(sqbuf.at[me], sqbuf.at[me], nss.at[i], nrs.at[me], blk=i))
+        start_if(i != me, remote(sqbuf.at[me], sqbuf.at[me], tss.at[i], nrs.at[me], blk=i))
     finish_s = gather(
-        sbuf, [(head, head)], sss, srs, n, me, forward=(head, sfs),
+        sbuf, [(0, 0), (1, 1)], gss, srs, n, me,
         visit=products(sbuf, ((gacc, gv), (acc, uv))),
     )
     for i in range(n):
-        pl.when(i != me)(remote(sqbuf.at[i], sqbuf.at[i], nss.at[i], nrs.at[i], blk=i).wait)
+        pl.when(i != me)(remote(sqbuf.at[i], sqbuf.at[i], tss.at[i], nrs.at[i], blk=i).wait)
     spread = lax.dot_general(
         jnp.sum(sqbuf[...], axis=0), jnp.full((8, gacc.shape[1]), 0.125, F32), (((0,), (0,)), ((), ())),
         precision=lax.Precision.HIGHEST, preferred_element_type=F32,
@@ -440,11 +439,10 @@
     hbuf[0, me] = hidden[:, :cut]
     hbuf[1, me] = hidden[:, cut:]
     acc[...] = jnp.zeros_like(acc)
-    finish_h = gather(hbuf, [(0, 0), (1, 1)], hss, hrs, n, me, visit=products(hbuf, ((acc, dv),)))
+    finish_s()
+    finish_h = gather(hbuf, [(0, 0), (1, 1)], gss, hrs, n, me, visit=products(hbuf, ((acc, dv),)))
     down = swap(acc[...], mine.at[1], theirs.at[1], xss.at[1], xrs.at[1], head)
     out[...] = (stream[...] + down).astype(BF)
-    finish_a()
-    finish_s()
     finish_h()
 
 
@@ -497,8 +495,8 @@
             pltpu.VMEM((2, rows, cols), BF),
             pltpu.VMEM((2, rows, cols), BF),
             DMA((2, s)), DMA((2, n)), DMA((batch, n)), DMA((batch, n)), DMA((n,)), DMA((n,)),
-            DMA((2, s)), DMA((2, n)), DMA((2, s)), DMA((2, n)), DMA((n,)), DMA((n,)), DMA((n,)),
-            DMA((2, s)), DMA((2, n)), DMA((2 + batch,)), DMA((4,)), DMA((2,)), DMA((2,)),
+            DMA((2, n)), DMA((2, n)), DMA((n,)), DMA((2, n)),
+            DMA((2 + batch,)), DMA((4,)), DMA((2,)), DMA((2,)),
         ],
         compiler_params=pltpu.CompilerParams(
             collective_id=0, has_side_effects=True, vmem_limit_bytes=67_043_328

time: 124 us -> 119 us (0.960)
  Pallas kernels: 121 us -> 116 us
    pallas_call x1, Pallas kernels: 121 us -> 116 us  [kernel_body(): pl.pallas_call(functools.partial(layer, n), out_shape=jax.ShapeDtypeStruc...]
where the time goes in v3:
time: 119 us
  Pallas kernels  116 us (97%)
  local copies, waits for them, and re-layouts  2.83 us (2%)
    pallas_call x1, Pallas kernels, kernel_body(): pl.pallas_call(functools.partial(layer, n), out_shape=jax.ShapeDtypeStruc...  116 us

profile of v3, /device:TPU:0, one launch (start us, length us, event | category | flops | bytes accessed | tf_op | source)
XLA Modules:
  0.0 118.8 jit_solution(7861411415562163553)
XLA Ops:
  0.0 1.3 %reshape.11.gain = bf16[1,512]{1,0:T(2,128)(2,1)} reshape(bf16[512]{0:T(512)(128)(2,1)} %param.16) | data formatting | bytes 2048 | tf_op jit(solution)/shard_map/reshape | solution.py:506
  1.3 116.0 %layer.1 = bf16[128,512]{1,0:T(8,128)(2,1)} custom-call(s32[2]{0:T(128)} %lengths.1, bf16[8,4096]{1,0:T(8,128)(2,1)} %q.1, bf16[2,8192,128]{2,1,0:T(8,128)(2,1)} %bitcast.2, bf16[2,8192,128]{2,1,0:T(8,128)(2,1)} %bitcast.3, bf16[128,512]{1,0:T(8,128)(2,1)} %residual.1, bf16[1,512]{1,0:T(2,128)(2,1)} %reshape.11.gain, bf16[4096,512]{1,0:T(8,128)(2,1)} %ow.1, ...), custom_call_target="tpu_custom_call" | custom-call | tf_op jit(solution)/shard_map/layer/pallas_call | solution.py:467
  117.3 1.6 %copy.12 = bf16[128,512]{1,0:T(8,128)(2,1)} copy(bf16[128,512]{1,0:T(8,128)(2,1)} %layer.1) | data formatting | bytes 262144
